TPU v7x, 32 devices: a whole 2x2x4 slice. The times are simulated.
32 devices in a mesh: gx: 8 (over z, y), gy: 4 (over x, core).
Axes of the slice: x: 2, y: 2, z: 4, core: 2. Of those that a mesh axis runs over, the one named last changes fastest.
Arguments:
- block_input: bfloat16 [960, 8192], P('gx', 'gy'), may hold values from -6 to 6
- attn_gain: float32 [960], P('gx'), may hold values from 0.5 to 1.5
- query_weight: bfloat16 [960, 960], P('gx', 'gy'), may hold values from -2 to 2
- key_weight: bfloat16 [960, 320], P('gx', 'gy'), may hold values from -2 to 2
- value_weight: bfloat16 [960, 320], P('gx', 'gy'), may hold values from -0.1875 to 0.1875
- output_weight: bfloat16 [960, 960], P('gy', 'gx'), may hold values from -0.5 to 0.5
- ffn_gain: float32 [960], P('gx'), may hold values from 0.5 to 1.5
- gate_weight: bfloat16 [960, 2560], P('gx', 'gy'), may hold values from -0.1875 to 0.1875
- up_weight: bfloat16 [960, 2560], P('gx', 'gy'), may hold values from -0.1875 to 0.1875
- down_weight: bfloat16 [2560, 960], P('gy', 'gx'), may hold values from -0.125 to 0.125
- segment_ids: int32 [8, 1024], P('gx'), may hold values from 0 to 7, never falling along the last dimension, each value on 1 to 512 neighbouring positions
- out_cotangent: bfloat16 [960, 8192], P('gx', 'gy'), may hold values from -6 to 6
Outputs:
- block_output: bfloat16 [960, 8192], P('gx', 'gy')
- input_grad: float32 [960, 8192], P('gx', 'gy')
- grad_attngain: float32 [960], P('gx')
- grad_query: float32 [960, 960], P('gx', 'gy')
- grad_key: float32 [960, 320], P('gx', 'gy')
- grad_value: float32 [960, 320], P('gx', 'gy')
- grad_outproj: float32 [960, 960], P('gy', 'gx')
- grad_ffngain: float32 [960], P('gx')
- grad_gate: float32 [960, 2560], P('gx', 'gy')
- grad_up: float32 [960, 2560], P('gx', 'gy')
- grad_down: float32 [2560, 960], P('gy', 'gx')
Inputs may be any that keep to these rules, and one draw needn't show every extreme that they name: `segment_ids`: along each packed sequence the numbers never fall.
All inputs are finite; a program needn't handle non-finite values.
Results may differ from a plain program's by a relative error of at most 0.023.
The roundings to bfloat16 on the way count: a program that leaves them out, or rounds other values in their place, can miss the bound.
Values may be sent and summed in bfloat16 or wider, within the bound.
A program may use at most 256 MiB of HBM per device.

v0:
```python
import math
import jax
import jax.numpy as jnp
from jax import lax
from jax.sharding import PartitionSpec as P

D = 960
QUERY_HEADS = 15
KEY_VALUE_HEADS = 5
HEAD_SIZE = 64
PACKED_LENGTH = 1024
EPS = 1e-05
THETA = 10000.0


def product(left, right):
    return jnp.dot(
        left.astype(jnp.float32),
        right.astype(jnp.float32),
        preferred_element_type=jnp.float32,
        precision=lax.Precision.HIGHEST,
    )


def einsum_full(form, left, right):
    return jnp.einsum(
        form, left.astype(jnp.float32), right.astype(jnp.float32), precision=lax.Precision.HIGHEST
    )


def segment_positions(segments):
    row_index = jnp.arange(segments.shape[1], dtype=jnp.int32)[None, :]
    starts = jnp.concatenate(
        [jnp.ones((segments.shape[0], 1), dtype=jnp.bool_), segments[:, 1:] != segments[:, :-1]],
        axis=1,
    )
    seg_first = lax.cummax(jnp.where(starts, row_index, jnp.zeros_like(row_index)), axis=1)
    return row_index - seg_first


def rope_tables(positions, half_dim):
    frequency = jnp.exp(-math.log(THETA) * jnp.arange(half_dim, dtype=jnp.float32) / half_dim)
    angles = positions.astype(jnp.float32)[:, None] * frequency[None, :]
    return (jnp.cos(angles)[:, None, :], jnp.sin(angles)[:, None, :])


def rotate(values, cos_table, sine_table, rotate_direction):
    n_rows = values.shape[0]
    half_dim = cos_table.shape[-1]
    split_heads = values.reshape(n_rows, -1, 2 * half_dim)
    lower_half = split_heads[..., :half_dim]
    upper_half = split_heads[..., half_dim:]
    new_lower = lower_half * cos_table - rotate_direction * upper_half * sine_table
    new_upper = upper_half * cos_table + rotate_direction * lower_half * sine_table
    return jnp.concatenate([new_lower, new_upper], axis=-1).reshape(n_rows, -1)


def contract_rows(left_rows, right_rows):
    return product(left_rows.T, right_rows)


def width_sum(values):
    return lax.psum(values, "gx")


def norm_forward(values, gain):
    scale = lax.rsqrt(width_sum(jnp.sum(values * values, axis=1)) / D + EPS)
    return (scale, (values * scale[:, None] * gain[None, :]).astype(jnp.bfloat16))


def norm_backward(values, scale, gain, grad_normed):
    weighted = grad_normed * gain[None, :]
    inner = width_sum(jnp.sum(weighted * values, axis=1)) / D
    grad_values = scale[:, None] * weighted - values * (scale * scale * scale * inner)[:, None]
    gain_part = jnp.sum(grad_normed * values * scale[:, None], axis=0)
    return (grad_values, gain_part)


def project_in(local_rows, weight):
    gathered = lax.all_gather(local_rows, "gy", axis=0, tiled=True)
    full_width = lax.all_to_all(gathered, "gx", split_axis=0, concat_axis=1, tiled=True)
    full_weight = lax.all_gather(weight, "gx", axis=0, tiled=True)
    return (gathered, product(full_width, full_weight))


def project_out(local_rows, weight):
    gathered = lax.all_gather(local_rows, "gx", axis=0, tiled=True)
    return (
        gathered,
        lax.psum_scatter(
            product(gathered, weight).astype(jnp.bfloat16), "gy", scatter_dimension=0, tiled=True
        ).astype(jnp.float32),
    )


def to_heads(columns):
    return lax.all_to_all(columns, "gy", split_axis=0, concat_axis=1, tiled=True)


def from_heads(block):
    return lax.all_to_all(block, "gy", split_axis=1, concat_axis=0, tiled=True)


def head_scores(query_per_head, key_per_head, allowed):
    scores = einsum_full("qkgd,ckd->kgqc", query_per_head, key_per_head) * HEAD_SIZE ** (-0.5)
    return jnp.where(allowed[None, None], scores, -jnp.inf)


def shards(
    block_input,
    attn_gain,
    query_weight,
    key_weight,
    value_weight,
    output_weight,
    ffn_gain,
    gate_weight,
    up_weight,
    down_weight,
    segment_ids,
    out_cotangent,
):
    resid_in = block_input.T.astype(jnp.float32)
    cot_local = out_cotangent.T
    scale_one, normed_one = norm_forward(resid_in, attn_gain)
    width_query = query_weight.shape[1]
    width_key = key_weight.shape[1]
    qkv_weight = jnp.concatenate([query_weight, key_weight, value_weight], axis=1)
    normed_one_rows, qkv_sums = project_in(normed_one, qkv_weight)
    qkv_raw = qkv_sums.astype(jnp.bfloat16)
    query_raw = qkv_raw[:, :width_query]
    key_raw = qkv_raw[:, width_query : width_query + width_key]
    value_raw = qkv_raw[:, width_query + width_key :]
    query_block = to_heads(query_raw)
    key_full, value_expanded = (
        lax.all_gather(key_raw, "gy", axis=1, tiled=True),
        lax.all_gather(value_raw, "gy", axis=1, tiled=True),
    )
    block_row_slab = query_block.shape[0]
    query_groups = QUERY_HEADS // KEY_VALUE_HEADS
    query_start = lax.axis_index("gy") * block_row_slab
    seq_start = query_start // PACKED_LENGTH * PACKED_LENGTH
    positions = segment_positions(segment_ids).reshape(-1)
    seg_flat = segment_ids.reshape(-1)
    cos_all, sine_all = rope_tables(positions, HEAD_SIZE // 2)
    cos_query = lax.dynamic_slice_in_dim(cos_all, query_start, block_row_slab, 0)
    sine_query = lax.dynamic_slice_in_dim(sine_all, query_start, block_row_slab, 0)
    key_rotated = rotate(key_full.astype(jnp.float32), cos_all, sine_all, 1.0).astype(jnp.bfloat16)
    query_rotated = rotate(query_block.astype(jnp.float32), cos_query, sine_query, 1.0).astype(
        jnp.bfloat16
    )
    seg_query = lax.dynamic_slice_in_dim(seg_flat, query_start, block_row_slab, 0)
    query_index = query_start - seq_start + jnp.arange(block_row_slab, dtype=jnp.int32)
    key_index = jnp.arange(PACKED_LENGTH, dtype=jnp.int32)
    allowed = (seg_query[:, None] == seg_flat[None, :]) & (
        key_index[None, :] <= query_index[:, None]
    )
    query_per_head = query_rotated.reshape(block_row_slab, KEY_VALUE_HEADS, query_groups, HEAD_SIZE)
    key_per_head = key_rotated.reshape(PACKED_LENGTH, KEY_VALUE_HEADS, HEAD_SIZE)
    value_per_head = value_expanded.reshape(PACKED_LENGTH, KEY_VALUE_HEADS, HEAD_SIZE)
    scores = head_scores(query_per_head, key_per_head, allowed)
    row_top = jnp.max(scores, axis=-1, keepdims=True)
    log_total = row_top + jnp.log(jnp.sum(jnp.exp(scores - row_top), axis=-1, keepdims=True))
    prob_half = jnp.exp(scores - log_total).astype(jnp.bfloat16)
    mixed = einsum_full("kgqc,ckd->qkgd", prob_half, value_per_head)
    attn_block = mixed.reshape(block_row_slab, -1).astype(jnp.bfloat16)
    attn_rows = from_heads(attn_block)
    attn_gathered, attn_sum = project_out(attn_rows, output_weight)
    hidden_in = resid_in + attn_sum
    scale_two, normed_two = norm_forward(hidden_in, ffn_gain)
    width_ff = gate_weight.shape[1]
    gate_up = jnp.concatenate([gate_weight, up_weight], axis=1)
    normed_two_rows, gate_sums = project_in(normed_two, gate_up)
    gate_pre = gate_sums[:, :width_ff]
    up_pre = gate_sums[:, width_ff:]
    hidden = (jax.nn.silu(gate_pre) * up_pre).astype(jnp.bfloat16)
    hidden_gathered, ffn_sum = project_out(hidden, down_weight)
    block_output = (hidden_in + ffn_sum).astype(jnp.bfloat16)
    cot_rows, hidden_grad = project_in(cot_local, down_weight.T)
    grad_down = contract_rows(lax.all_gather(hidden, "gx", axis=0, tiled=True), cot_rows)
    gate_sigmoid = jax.nn.sigmoid(gate_pre)
    gate_back = (
        hidden_grad * up_pre * gate_sigmoid * (1.0 + gate_pre * (1.0 - gate_sigmoid))
    ).astype(jnp.bfloat16)
    up_back = (hidden_grad * gate_pre * gate_sigmoid).astype(jnp.bfloat16)
    gate_up_rows, normed_two_grad = project_out(
        jnp.concatenate([gate_back, up_back], axis=1), gate_up.T
    )
    grad_gate_up = contract_rows(normed_two_rows, gate_up_rows)
    hidden_in_grad, gain_two_part = norm_backward(hidden_in, scale_two, ffn_gain, normed_two_grad)
    hidden_in_grad = hidden_in_grad + cot_local.astype(jnp.float32)
    hidden_in_half = hidden_in_grad.astype(jnp.bfloat16)
    grad_rows, attn_grad = project_in(hidden_in_half, output_weight.T)
    grad_outproj = contract_rows(attn_gathered, grad_rows)
    block_gradient = to_heads(attn_grad.astype(jnp.bfloat16))
    head_gradient = block_gradient.reshape(block_row_slab, KEY_VALUE_HEADS, query_groups, HEAD_SIZE)
    scores = head_scores(query_per_head, key_per_head, allowed)
    prob_full = jnp.exp(scores - log_total)
    prob_half = prob_full.astype(jnp.bfloat16)
    prob_grad = einsum_full("qkgd,ckd->kgqc", head_gradient, value_per_head)
    row_dot = jnp.sum(prob_full * prob_grad, axis=-1, keepdims=True)
    score_grad = (prob_full * (prob_grad - row_dot) * HEAD_SIZE ** (-0.5)).astype(jnp.bfloat16)
    query_grad = einsum_full("kgqc,ckd->qkgd", score_grad, key_per_head).reshape(block_row_slab, -1)
    key_grad = einsum_full("kgqc,qkgd->ckd", score_grad, query_per_head).reshape(PACKED_LENGTH, -1)
    value_grad = einsum_full("kgqc,qkgd->ckd", prob_half, head_gradient).reshape(PACKED_LENGTH, -1)
    query_back = rotate(query_grad, cos_query, sine_query, -1.0).astype(jnp.bfloat16)
    key_grad_all = rotate(key_grad, cos_all, sine_all, -1.0)
    key_back, value_back = (
        lax.psum_scatter(
            key_grad_all.astype(jnp.bfloat16), "gy", scatter_dimension=1, tiled=True
        ).astype(jnp.float32),
        lax.psum_scatter(
            value_grad.astype(jnp.bfloat16), "gy", scatter_dimension=1, tiled=True
        ).astype(jnp.float32),
    )
    query_cols = from_heads(query_back)
    qkv_grad = jnp.concatenate(
        [query_cols, key_back.astype(jnp.bfloat16), value_back.astype(jnp.bfloat16)], axis=1
    )
    qkv_grad_rows, normed_one_grad = project_out(qkv_grad, qkv_weight.T)
    grad_qkv = contract_rows(normed_one_rows, qkv_grad_rows)
    input_grad, gain_one_part = norm_backward(resid_in, scale_one, attn_gain, normed_one_grad)
    input_grad = input_grad + hidden_in_grad
    grad_attngain, grad_ffngain = lax.psum((gain_one_part, gain_two_part), "gy")
    grad_query = grad_qkv[:, :width_query]
    grad_key = grad_qkv[:, width_query : width_query + width_key]
    grad_value = grad_qkv[:, width_query + width_key :]
    grad_gate = grad_gate_up[:, :width_ff]
    grad_up = grad_gate_up[:, width_ff:]
    return (
        block_output.T,
        input_grad.T,
        grad_attngain,
        grad_query,
        grad_key,
        grad_value,
        grad_outproj,
        grad_ffngain,
        grad_gate,
        grad_up,
        grad_down,
    )


def solution(mesh):
    return jax.shard_map(
        shards,
        mesh=mesh,
        in_specs=(
            P("gx", "gy"),
            P("gx"),
            P("gx", "gy"),
            P("gx", "gy"),
            P("gx", "gy"),
            P("gy", "gx"),
            P("gx"),
            P("gx", "gy"),
            P("gx", "gy"),
            P("gy", "gx"),
            P("gx", None),
            P("gx", "gy"),
        ),
        out_specs=(
            P("gx", "gy"),
            P("gx", "gy"),
            P("gx"),
            P("gx", "gy"),
            P("gx", "gy"),
            P("gx", "gy"),
            P("gy", "gx"),
            P("gx"),
            P("gx", "gy"),
            P("gx", "gy"),
            P("gy", "gx"),
        ),
        check_vma=False,
    )
```

profile of v0, /device:TPU:0, one launch (start us, length us, event | category | flops | bytes accessed | tf_op | source)
XLA Modules:
  0.0 1488.6 jit_solution(9215844757252421216)
XLA Ops:
  8.4 23.4 %psum.42 = f32[2048]{0:T(1024)S(1)} all-reduce(f32[2048]{0:T(1024)S(1)} %fusion.35), channel_id=1, replica_groups=mesh['gx'=8,'gy'=4] {'gx'}, use_global_device_ids=true, to_apply=%region_1.0 | all-reduce | flops 2048 | bytes 16384 | tf_op jit(solution)/shard_map/psum | solution.py:63
  31.8 1.9 fusion.37
  33.8 19.2 %all-gather.12.cloned.1.call-done = bf16[8192,120]{0,1:T(8,128)(2,1)} async-done(((bf16[2048,120]{0,1:T(8,128)(2,1)}), bf16[8192,120]{0,1:T(8,128)(2,1)}) %all-gather.12.cloned.1.call-update) | async-done | bytes 1966096 | tf_op jit(solution)/shard_map/all_gather | solution.py:80
  53.0 3.0 copy.113
  56.0 5.7 all-to-all-start
  62.7 67.0 %all-gather = bf16[8,120,400]{1,2,0:T(8,128)(2,1)S(1)} all-gather(bf16[1,120,400]{1,2,0:T(8,128)(2,1)S(1)} %fusion.41), channel_id=1, replica_groups=mesh['gx'=8,'gy'=4] {'gx'}, dimensions={0}, use_global_device_ids=true | all-gather | bytes 864000 | tf_op jit(solution)/shard_map/all_gather | solution.py:82
  132.8 2.6 convolution_convert_fusion.4
  136.2 3.5 all-to-all-start.1
  139.8 12.8 all_gather.46
  152.5 8.0 all_gather.45
  161.1 6.8 fusion.52
  168.0 7.5 exponential_reduce_fusion
  175.5 8.0 fusion.16
  183.5 10.9 all_to_all.137
  195.3 68.4 %all-gather.14.cloned.1.call-done = bf16[8192,240]{0,1:T(8,128)(2,1)} async-done(((bf16[1024,240]{0,1:T(8,128)(2,1)}), bf16[8192,240]{0,1:T(8,128)(2,1)}) %all-gather.14.cloned.1.call-update) | async-done | bytes 3932176 | tf_op jit(solution)/shard_map/all_gather | solution.py:87
  263.7 4.1 convolution_convert_fusion
  268.4 28.6 %reduce-scatter.7.cloned.1.call-done = bf16[2048,120]{0,1:T(8,128)(2,1)} async-done(((bf16[8192,120]{0,1:T(8,128)(2,1)}), bf16[2048,120]{0,1:T(8,128)(2,1)}) %reduce-scatter.7.cloned.1.call-update) | async-done | bytes 491536 | tf_op jit(solution)/shard_map/reduce_scatter | solution.py:90
  298.3 21.7 %psum.43 = f32[2048]{0:T(1024)S(1)} all-reduce(f32[2048]{0:T(1024)S(1)} %multiply_reduce_fusion), channel_id=1, replica_groups=mesh['gx'=8,'gy'=4] {'gx'}, use_global_device_ids=true, to_apply=%region_8.9 | all-reduce | flops 2048 | bytes 16384 | tf_op jit(solution)/shard_map/psum | solution.py:63
  320.0 2.0 multiply_convert_fusion.3
  322.6 17.7 %all-gather.16.cloned.1.call-done = bf16[8192,120]{0,1:T(8,128)(2,1)} async-done(((bf16[2048,120]{0,1:T(8,128)(2,1)}), bf16[8192,120]{0,1:T(8,128)(2,1)}) %all-gather.16.cloned.1.call-update) | async-done | bytes 1966096 | tf_op jit(solution)/shard_map/all_gather | solution.py:80
  340.3 3.0 copy.112
  343.3 5.6 all-to-all-start.3
  349.8 13.8 all-gather.22.cloned.1.call-done
  363.5 3.1 copy.111
  366.6 38.2 %all-to-all-done.3 = bf16[8,1024,120]{1,2,0:T(8,128)(2,1)} async-done(((bf16[8,1024,120]{1,2,0:T(8,128)(2,1)}), bf16[8,1024,120]{1,2,0:T(8,128)(2,1)}, u32[]{:S(2)}, u32[]{:S(2)}) %all-to-all-start.3) | async-done | bytes 1966112 | tf_op jit(solution)/shard_map/all_to_all | solution.py:81
  404.8 4.3 all-to-all-start.4
  409.9 36.0 %all-gather.18.cloned.1.call-done = bf16[960,1280]{1,0:T(8,128)(2,1)} async-done(((bf16[120,1280]{1,0:T(8,128)(2,1)}), bf16[960,1280]{1,0:T(8,128)(2,1)}) %all-gather.18.cloned.1.call-update) | async-done | bytes 2457616 | tf_op jit(solution)/shard_map/all_gather | solution.py:82
  445.9 7.5 fusion.53
  453.4 45.1 %all-gather.24.cloned.1.call-done = bf16[960,640]{1,0:T(8,128)(2,1)} async-done(((bf16[120,640]{1,0:T(8,128)(2,1)}), bf16[960,640]{1,0:T(8,128)(2,1)}) %all-gather.24.cloned.1.call-update) | async-done | bytes 1228816 | tf_op jit(solution)/shard_map/all_gather | solution.py:82
  498.5 7.3 multiply_convert_fusion.1
  505.9 1.7 pad_maximum_fusion
  507.6 400.4 %all-gather.26.cloned.1.call-done = bf16[8192,1280]{1,0:T(8,128)(2,1)} async-done(((bf16[1024,1280]{1,0:T(8,128)(2,1)}), bf16[8192,1280]{1,0:T(8,128)(2,1)}) %all-gather.26.cloned.1.call-update) | async-done | bytes 20971536 | tf_op jit(solution)/shard_map/all_gather | solution.py:87
  908.0 14.8 convolution_convert_fusion.3
  922.9 30.5 %reduce-scatter.11.cloned.1.call-done = bf16[2048,120]{0,1:T(8,128)(2,1)} async-done(((bf16[8192,120]{0,1:T(8,128)(2,1)}), bf16[2048,120]{0,1:T(8,128)(2,1)}) %reduce-scatter.11.cloned.1.call-update) | async-done | bytes 491536 | tf_op jit(solution)/shard_map/reduce_scatter | solution.py:90
  953.4 2.0 fusion.32
  955.4 22.4 %psum.44 = f32[2048]{0:T(1024)} all-reduce(f32[2048]{0:T(1024)S(1)} %get-tuple-element.56), channel_id=1, replica_groups=mesh['gx'=8,'gy'=4] {'gx'}, use_global_device_ids=true, to_apply=%region_12.13 | all-reduce | flops 2048 | bytes 16384 | tf_op jit(solution)/shard_map/psum | solution.py:63
  978.6 2.2 fusion.40
  980.8 18.3 %all-gather.28.cloned.1.call-done = bf16[8192,120]{0,1:T(8,128)(2,1)} async-done(((bf16[2048,120]{0,1:T(8,128)(2,1)}), bf16[8192,120]{0,1:T(8,128)(2,1)}) %all-gather.28.cloned.1.call-update) | async-done | bytes 1966096 | tf_op jit(solution)/shard_map/all_gather | solution.py:80
  999.1 3.0 copy.110
  1002.1 5.5 all-to-all-start.5
  1007.6 1.6 copy.80
  1009.2 67.3 %all_gather.55 = bf16[960,240]{1,0:T(8,128)(2,1)} all-gather(bf16[120,240]{1,0:T(8,128)(2,1)} %bitcast.221), channel_id=1, replica_groups=mesh['gx'=8,'gy'=4] {'gx'}, dimensions={0}, use_global_device_ids=true | all-gather | bytes 518400 | tf_op jit(solution)/shard_map/all_gather | solution.py:82
  1076.5 2.3 convolution_convert_fusion.5
  1078.8 10.9 all_to_all.138
  1089.7 8.9 fusion.13
  1098.6 7.8 fusion.54
  1106.4 25.3 %fusion.3 = bf16[5,3,256,1024]{2,3,1,0:T(8,128)(2,1)} fusion(f32[5,1024,256,3]{2,1,3,0:T(8,128)} %fusion.54, f32[5,3,256,1024]{2,3,1,0:T(8,128)} %get-tuple-element.86, f32[5,3,256]{2,1,0:T(4,128)S(1)} %log_add_fusion), kind=kOutput, calls=%fused_computation.5 | output fusion | flops 27529984 | bytes 39336960 | tf_op jit(solution)/shard_map/sub | solution.py:202
  1131.7 5.7 convolution_bitcast_fusion
  1138.6 4.7 fusion.39
  1143.5 10.9 all_to_all.139
  1154.4 5.2 reduce-scatter.13.cloned.1.call-done
  1159.6 1.9 pad_maximum_fusion.1
  1162.4 101.9 %all-gather.30.cloned.1.call-done = bf16[8192,400]{0,1:T(8,128)(2,1)} async-done(((bf16[1024,400]{0,1:T(8,128)(2,1)}), bf16[8192,400]{0,1:T(8,128)(2,1)}) %all-gather.30.cloned.1.call-update) | async-done | bytes 6553616 | tf_op jit(solution)/shard_map/all_gather | solution.py:87
  1264.3 5.4 convolution_convert_fusion.1
  1269.8 145.3 %all-gather.20.cloned.1.call-done = bf16[8192,640]{1,0:T(8,128)(2,1)} async-done(((bf16[1024,640]{1,0:T(8,128)(2,1)}), bf16[8192,640]{1,0:T(8,128)(2,1)}) %all-gather.20.cloned.1.call-update) | async-done | bytes 10485776 | tf_op jit(solution)/shard_map/all_gather | solution.py:87
  1415.0 9.3 convolution_convert_fusion.2
  1424.4 7.2 fusion.58
  1431.6 8.9 fusion.57
  1441.4 1.8 fusion.56
  1443.2 1.9 fusion.55
  1448.1 6.8 all-reduce
  1454.8 20.8 %psum.45 = f32[2048]{0:T(1024)S(1)} all-reduce(f32[2048]{0:T(1024)S(1)} %get-tuple-element.58), channel_id=1, replica_groups=mesh['gx'=8,'gy'=4] {'gx'}, use_global_device_ids=true, to_apply=%region_18.19 | all-reduce | flops 2048 | bytes 16384 | tf_op jit(solution)/shard_map/psum | solution.py:63
  1475.6 3.3 reduce-scatter.9.cloned.1.call-done
  1478.9 3.0 fusion.26
  (145 shorter events, 18.7 us)
Async XLA Ops:
  7.2 45.8 %all-gather.12.cloned.1.call-start = ((), (), s32[]{:S(2)}) async-start(), calls=%async_computation.14 | async-start | bytes 2457600 | tf_op jit(solution)/shard_map/all_gather | solution.py:80
  56.0 5.7 copy-start.22
  56.0 6.5 copy-start.21
  56.0 6.6 copy-start.16
  56.0 6.6 copy-start.18
  56.0 76.8 %all-to-all-start = ((bf16[8,1024,120]{1,2,0:T(8,128)(2,1)}), bf16[8,1024,120]{1,2,0:T(8,128)(2,1)}, u32[]{:S(2)}, u32[]{:S(2)}) async-start(bf16[8,1024,120]{1,2,0:T(8,128)(2,1)} %bitcast.187), calls=%async_computation | async-start | bytes 3932160 | tf_op jit(solution)/shard_map/all_to_all | solution.py:81
  136.2 24.6 %all-to-all-start.1 = ((bf16[4,256,240]{1,2,0:T(8,128)(2,1)}), bf16[4,256,240]{1,2,0:T(8,128)(2,1)S(1)}, u32[]{:S(2)}, u32[]{:S(2)}) async-start(bf16[4,256,240]{1,2,0:T(8,128)(2,1)} %bitcast.189), calls=%async_computation.1 | async-start | bytes 983040 | tf_op jit(solution)/shard_map/all_to_all | solution.py:97
  139.7 124.0 %all-gather.14.cloned.1.call-start = ((), (), s32[]{:S(2)}) async-start(), calls=%async_computation.15 | async-start | bytes 4423680 | tf_op jit(solution)/shard_map/all_gather | solution.py:87
  175.5 88.2 %copy-start.12 = (bf16[240,120]{1,0:T(8,128)(2,1)S(1)}, bf16[240,120]{1,0:T(8,128)(2,1)}, u32[]{:S(2)}) copy-start(bf16[240,120]{1,0:T(8,128)(2,1)} %param.17) | copy-start | bytes 172804
  195.3 101.8 %copy-start = (bf16[120,2048]{1,0:T(8,128)(2,1)S(1)}, bf16[120,2048]{1,0:T(8,128)(2,1)}, u32[]{:S(2)}) copy-start(bf16[120,2048]{1,0:T(8,128)(2,1)} %param.12) | copy-start | bytes 1474564
  195.3 101.8 %reduce-scatter.7.cloned.1.call-start = ((), (), s32[]{:S(2)}) async-start(), calls=%async_computation.16 | async-start | bytes 2457600 | tf_op jit(solution)/shard_map/reduce_scatter | solution.py:90
  267.9 52.1 %copy-start.23 = (f32[120]{0:T(128)S(1)}, f32[120]{0:T(128)}, u32[]{:S(2)}) copy-start(f32[120]{0:T(128)} %param.18) | copy-start | bytes 1444
  267.9 72.4 %all-gather.16.cloned.1.call-start = ((), (), s32[]{:S(2)}) async-start(), calls=%async_computation.17 | async-start | bytes 2457600 | tf_op jit(solution)/shard_map/all_gather | solution.py:80
  320.0 23.3 %copy-start.20 = (f32[2048]{0:T(1024)}, f32[2048]{0:T(1024)S(1)}, u32[]{:S(2)}) copy-start(f32[2048]{0:T(1024)S(1)} %psum.43) | copy-start | bytes 24580
  322.0 41.5 %all-gather.22.cloned.1.call-start = ((), (), s32[]{:S(2)}) async-start(), calls=%async_computation.21 | async-start | bytes 2457600 | tf_op jit(solution)/shard_map/all_gather | solution.py:80
  343.3 5.7 copy-start.13
  343.3 5.7 copy-start.14
  343.3 61.5 %all-to-all-start.3 = ((bf16[8,1024,120]{1,2,0:T(8,128)(2,1)}), bf16[8,1024,120]{1,2,0:T(8,128)(2,1)}, u32[]{:S(2)}, u32[]{:S(2)}) async-start(bf16[8,1024,120]{1,2,0:T(8,128)(2,1)} %bitcast.198), calls=%async_computation.4 | async-start | bytes 3932160 | tf_op jit(solution)/shard_map/all_to_all | solution.py:81
  348.9 97.0 %all-gather.18.cloned.1.call-start = ((), (), s32[]{:S(2)}) async-start(), calls=%async_computation.18 | async-start | bytes 2764800 | tf_op jit(solution)/shard_map/all_gather | solution.py:82
  349.0 0.7 copy-start.8
  404.8 93.8 %all-to-all-start.4 = ((bf16[8,1024,120]{1,2,0:T(8,128)(2,1)}), bf16[8,1024,120]{1,2,0:T(8,128)(2,1)}, u32[]{:S(2)}, u32[]{:S(2)}) async-start(bf16[8,1024,120]{1,2,0:T(8,128)(2,1)} %bitcast.197), calls=%async_computation.6 | async-start | bytes 3932160 | tf_op jit(solution)/shard_map/all_to_all | solution.py:81
  409.1 89.4 %all-gather.24.cloned.1.call-start = ((), (), s32[]{:S(2)}) async-start(), calls=%async_computation.22 | async-start | bytes 1382400 | tf_op jit(solution)/shard_map/all_gather | solution.py:82
  409.9 498.1 %all-gather.26.cloned.1.call-start = ((), (), s32[]{:S(2)}) async-start(), calls=%async_computation.23 | async-start | bytes 23592960 | tf_op jit(solution)/shard_map/all_gather | solution.py:87
  507.5 400.5 %copy-start.9 = (bf16[120,1280]{1,0:T(8,128)(2,1)S(1)}, bf16[120,1280]{1,0:T(8,128)(2,1)}, u32[]{:S(2)}) copy-start(bf16[120,1280]{1,0:T(8,128)(2,1)} %copy-done.8) | copy-start | bytes 921604
  507.5 445.9 %copy-start.3 = (bf16[2048,120]{0,1:T(8,128)(2,1)S(1)}, bf16[2048,120]{0,1:T(8,128)(2,1)}, u32[]{:S(2)}) copy-start(bf16[2048,120]{0,1:T(8,128)(2,1)} %reduce-scatter.7.cloned.1.call-done) | copy-start | bytes 1474564
  507.5 445.8 %reduce-scatter.11.cloned.1.call-start = ((), (), s32[]{:S(2)}) async-start(), calls=%async_computation.24 | async-start | bytes 2457600 | tf_op jit(solution)/shard_map/reduce_scatter | solution.py:90
  922.8 55.8 %copy-start.6 = (bf16[120,2048]{1,0:T(8,128)(2,1)S(1)}, bf16[120,2048]{1,0:T(8,128)(2,1)}, u32[]{:S(2)}) copy-start(bf16[120,2048]{1,0:T(8,128)(2,1)} %param.23) | copy-start | bytes 1474564
  922.8 76.2 %all-gather.28.cloned.1.call-start = ((), (), s32[]{:S(2)}) async-start(), calls=%async_computation.25 | async-start | bytes 2457600 | tf_op jit(solution)/shard_map/all_gather | solution.py:80
  1002.1 74.4 %all-to-all-start.5 = ((bf16[8,1024,120]{1,2,0:T(8,128)(2,1)}), bf16[8,1024,120]{1,2,0:T(8,128)(2,1)}, u32[]{:S(2)}, u32[]{:S(2)}) async-start(bf16[8,1024,120]{1,2,0:T(8,128)(2,1)} %bitcast.199), calls=%async_computation.8 | async-start | bytes 3932160 | tf_op jit(solution)/shard_map/all_to_all | solution.py:81
  1007.6 146.8 %reduce-scatter.15.cloned.1.call-start = ((), (), s32[]{:S(2)}) async-start(), calls=%async_computation.27 | async-start | bytes 819200 | tf_op jit(solution)/shard_map/reduce_scatter | solution.py:212
  1106.3 53.2 %reduce-scatter.13.cloned.1.call-start = ((), (), s32[]{:S(2)}) async-start(), calls=%async_computation.26 | async-start | bytes 819200 | tf_op jit(solution)/shard_map/reduce_scatter | solution.py:209
  1131.7 5.7 copy-start.11
  1138.5 4.7 copy-start.15
  1138.5 125.7 %all-gather.30.cloned.1.call-start = ((), (), s32[]{:S(2)}) async-start(), calls=%async_computation.28 | async-start | bytes 7372800 | tf_op jit(solution)/shard_map/all_gather | solution.py:87
  1154.3 110.0 %copy-start.17 = (bf16[120,80]{0,1:T(8,128)(2,1)S(1)}, bf16[120,80]{0,1:T(8,128)(2,1)}, u32[]{:S(2)}) copy-start(bf16[120,80]{0,1:T(8,128)(2,1)} %param.16) | copy-start | bytes 57604
  1154.3 110.0 %copy-start.19 = (bf16[120,80]{0,1:T(8,128)(2,1)S(1)}, bf16[120,80]{0,1:T(8,128)(2,1)}, u32[]{:S(2)}) copy-start(bf16[120,80]{0,1:T(8,128)(2,1)} %param.15) | copy-start | bytes 57604
  1161.5 253.5 %all-gather.20.cloned.1.call-start = ((), (), s32[]{:S(2)}) async-start(), calls=%async_computation.19 | async-start | bytes 11796480 | tf_op jit(solution)/shard_map/all_gather | solution.py:87
  1162.1 252.9 %copy-start.10 = (bf16[640,120]{0,1:T(8,128)(2,1)S(1)}, bf16[640,120]{0,1:T(8,128)(2,1)}, u32[]{:S(2)}) copy-start(bf16[640,120]{0,1:T(8,128)(2,1)} %param.21) | copy-start | bytes 460804
  1162.1 284.4 %reduce-scatter.17.cloned.1.call-start = ((), (), s32[]{:S(2)}) async-start(), calls=%async_computation.29 | async-start | bytes 2457600 | tf_op jit(solution)/shard_map/reduce_scatter | solution.py:90
  1269.7 209.2 %reduce-scatter.9.cloned.1.call-start = ((), (), s32[]{:S(2)}) async-start(), calls=%async_computation.20 | async-start | bytes 2457600 | tf_op jit(solution)/shard_map/reduce_scatter | solution.py:90
  1424.4 7.2 copy-start.4
  1424.4 18.8 %slice-start = ((s8[6553600]{0:T(1024)(128)(4,1)}), s8[4194304]{0:T(1024)(128)(4,1)S(1)}, s32[]{:S(2)}) async-start(s8[6553600]{0:T(1024)(128)(4,1)} %bitcast.190), calls=%async_computation.30 | async-start | bytes 8388608
  1431.6 9.8 copy-start.1
  1431.6 9.8 copy-start.5
  1431.6 11.6 slice-start.1
  1441.4 1.8 copy-start.2
  1443.2 3.4 copy-start.25
  1443.2 4.8 copy-start.26
  1443.2 35.7 %copy-start.7 = (bf16[2048,120]{0,1:T(8,128)(2,1)S(1)}, bf16[2048,120]{0,1:T(8,128)(2,1)}, u32[]{:S(2)}) copy-start(bf16[2048,120]{0,1:T(8,128)(2,1)} %reduce-scatter.11.cloned.1.call-done) | copy-start | bytes 1474564
  1443.2 35.7 %copy-start.24 = (f32[120]{0:T(128)S(1)}, f32[120]{0:T(128)}, u32[]{:S(2)}) copy-start(f32[120]{0:T(128)} %param.18) | copy-start | bytes 1444
Sparse Core Ops, SparseCore 0:
  33.9 19.0 all-gather.11
  195.4 68.2 all-gather.13
  268.0 28.9 reduce-scatter.6
  322.1 18.0 all-gather.15
  341.7 21.8 all-gather.21
  366.1 79.7 all-gather.17
  448.1 50.4 all-gather.23
  507.7 400.3 all-gather.25
  923.0 30.3 reduce-scatter.10
  980.9 18.1 all-gather.27
  1106.5 20.9 reduce-scatter.14
  1138.6 20.8 reduce-scatter.12
  1162.3 101.8 all-gather.29
  1266.3 148.6 all-gather.19
  1417.5 28.5 reduce-scatter.16
  1448.5 30.3 reduce-scatter.8
where the time goes:
time: 1500 us; the launch traced here: 1490 us
  waiting for transfers between devices  974 us (65%)
  blocking collectives  283 us (19%)
  matrix products  115 us (8%)
  other arithmetic  56.8 us (4%)
  starting transfers between devices  26 us (2%)
  local copies, waits for them, and re-layouts  19.8 us (1%)
    all_gather x4, waiting for transfers between devices, project_out(): gathered = lax.all_gather(local_rows, 'gx', axis=0, tiled=True)  716 us
    all_gather x2, blocking collectives, project_in(): full_weight = lax.all_gather(weight, 'gx', axis=0, tiled=True)  134 us
    psum x4, blocking collectives, width_sum(): return lax.psum(values, 'gx')  88.3 us
    all_gather x2, waiting for transfers between devices, project_in(): full_weight = lax.all_gather(weight, 'gx', axis=0, tiled=True)  81.1 us
    dot_general x12, matrix products, product(): jnp.dot(left.astype(jnp.float32), right.astype(jnp.float32), preferred_el...  73.2 us
    all_gather x4, waiting for transfers between devices, project_in(): gathered = lax.all_gather(local_rows, 'gy', axis=0, tiled=True)  68.9 us
    reduce_scatter x4, waiting for transfers between devices, project_out(): lax.psum_scatter(product(gathered, weight).astype(jnp.bfloat16), 'gy', sc...  62.4 us
    dot_general x6, matrix products, einsum_full(): jnp.einsum(form, left.astype(jnp.float32), right.astype(jnp.float32), pre...  41.8 us
  transfers between devices with their start and end apart: 21, of which 15 were waited for; matrix products, arithmetic and copies ran while one was open for 6% of the time, Pallas kernels for 0%

commit v1 on v0

--- a/solution.py
+++ b/solution.py
@@ -60,7 +60,7 @@
 
 
 def width_sum(values):
-    return lax.psum(values, "gx")
+    return jnp.sum(lax.all_gather(values, "gx"), axis=0)
 
 
 def norm_forward(values, gain):

time: 1500 us -> 1550 us (1.033)
  blocking collectives: 283 us -> 320 us
    all_gather x0 -> x4, blocking collectives: none -> 126 us  [width_sum(): return jnp.sum(lax.all_gather(values, 'gx'), axis=0)]
    psum x4 -> x0, blocking collectives: 88.3 us -> none  [width_sum(): return lax.psum(values, 'gx')]
  transfers between devices with their start and end apart: 21 -> 21, of which waited for: 15 -> 14; matrix products, arithmetic and copies ran while one was open for 6% -> 6% of each run, Pallas kernels for 0% -> 0%
where the time goes in v1:
time: 1550 us; the launch traced here: 1540 us
  waiting for transfers between devices  981 us (63%)
  blocking collectives  320 us (21%)
  matrix products  115 us (7%)
  other arithmetic  58.3 us (4%)
  starting transfers between devices  26.1 us (2%)
  local copies, waits for them, and re-layouts  21.3 us (1%)
    all_gather x4, waiting for transfers between devices, project_out(): gathered = lax.all_gather(local_rows, 'gx', axis=0, tiled=True)  716 us
    all_gather x2, blocking collectives, project_in(): full_weight = lax.all_gather(weight, 'gx', axis=0, tiled=True)  134 us
    all_gather x4, blocking collectives, width_sum(): return jnp.sum(lax.all_gather(values, 'gx'), axis=0)  126 us
    all_gather x2, waiting for transfers between devices, project_in(): full_weight = lax.all_gather(weight, 'gx', axis=0, tiled=True)  81.1 us
    all_gather x4, waiting for transfers between devices, project_in(): gathered = lax.all_gather(local_rows, 'gy', axis=0, tiled=True)  79.9 us
    dot_general x12, matrix products, product(): jnp.dot(left.astype(jnp.float32), right.astype(jnp.float32), preferred_el...  73.2 us
    reduce_scatter x4, waiting for transfers between devices, project_out(): lax.psum_scatter(product(gathered, weight).astype(jnp.bfloat16), 'gy', sc...  59.5 us
    dot_general x6, matrix products, einsum_full(): jnp.einsum(form, left.astype(jnp.float32), right.astype(jnp.float32), pre...  41.8 us
  transfers between devices with their start and end apart: 21, of which 14 were waited for; matrix products, arithmetic and copies ran while one was open for 6% of the time, Pallas kernels for 0%

profile of v1, /device:TPU:0, one launch (start us, length us, event | category | flops | bytes accessed | tf_op | source)
XLA Modules:
  0.0 1536.6 jit_solution(5018626054229320383)
XLA Ops:
  8.4 32.4 %all-gather = f32[16384]{0:T(1024)S(1)} all-gather(f32[2048]{0:T(1024)S(1)} %fusion.35), channel_id=2, replica_groups=mesh['gx'=8,'gy'=4] {'gx'}, dimensions={0}, use_global_device_ids=true | all-gather | bytes 73728 | tf_op jit(solution)/shard_map/all_gather | solution.py:63
  40.8 1.9 fusion.37
  42.8 22.9 %all-gather.16.cloned.1.call-done = bf16[8192,120]{0,1:T(8,128)(2,1)} async-done(((bf16[2048,120]{0,1:T(8,128)(2,1)}), bf16[8192,120]{0,1:T(8,128)(2,1)}) %all-gather.16.cloned.1.call-update) | async-done | bytes 1966096 | tf_op jit(solution)/shard_map/all_gather | solution.py:80
  65.6 3.0 copy.131
  68.7 5.7 all-to-all-start
  75.3 67.0 %all-gather.4 = bf16[8,120,400]{1,2,0:T(8,128)(2,1)S(1)} all-gather(bf16[1,120,400]{1,2,0:T(8,128)(2,1)S(1)} %fusion.41), channel_id=1, replica_groups=mesh['gx'=8,'gy'=4] {'gx'}, dimensions={0}, use_global_device_ids=true | all-gather | bytes 864000 | tf_op jit(solution)/shard_map/all_gather | solution.py:82
  145.4 2.6 convolution_convert_fusion.4
  148.9 3.5 all-to-all-start.1
  152.4 12.8 all_gather.72
  165.2 8.0 all_gather.71
  173.8 6.8 fusion.52
  180.6 7.5 exponential_reduce_fusion
  188.2 8.0 fusion.16
  196.2 10.9 all_to_all.137
  208.4 67.9 %all-gather.18.cloned.1.call-done = bf16[8192,240]{0,1:T(8,128)(2,1)} async-done(((bf16[1024,240]{0,1:T(8,128)(2,1)}), bf16[8192,240]{0,1:T(8,128)(2,1)}) %all-gather.18.cloned.1.call-update) | async-done | bytes 3932176 | tf_op jit(solution)/shard_map/all_gather | solution.py:87
  276.4 4.1 convolution_convert_fusion
  280.6 29.1 %reduce-scatter.7.cloned.1.call-done = bf16[2048,120]{0,1:T(8,128)(2,1)} async-done(((bf16[8192,120]{0,1:T(8,128)(2,1)}), bf16[2048,120]{0,1:T(8,128)(2,1)}) %reduce-scatter.7.cloned.1.call-update) | async-done | bytes 491536 | tf_op jit(solution)/shard_map/reduce_scatter | solution.py:90
  310.9 30.6 %all-gather.1 = f32[16384]{0:T(1024)S(1)} all-gather(f32[2048]{0:T(1024)S(1)} %multiply_reduce_fusion), channel_id=3, replica_groups=mesh['gx'=8,'gy'=4] {'gx'}, dimensions={0}, use_global_device_ids=true | all-gather | bytes 73728 | tf_op jit(solution)/shard_map/all_gather | solution.py:63
  341.6 2.0 multiply_convert_fusion.3
  344.2 21.3 %all-gather.20.cloned.1.call-done = bf16[8192,120]{0,1:T(8,128)(2,1)} async-done(((bf16[2048,120]{0,1:T(8,128)(2,1)}), bf16[8192,120]{0,1:T(8,128)(2,1)}) %all-gather.20.cloned.1.call-update) | async-done | bytes 1966096 | tf_op jit(solution)/shard_map/all_gather | solution.py:80
  365.5 3.0 copy.130
  368.5 5.6 all-to-all-start.3
  375.0 13.8 all-gather.26.cloned.1.call-done
  388.8 3.1 copy.129
  391.9 38.2 %all-to-all-done.3 = bf16[8,1024,120]{1,2,0:T(8,128)(2,1)} async-done(((bf16[8,1024,120]{1,2,0:T(8,128)(2,1)}), bf16[8,1024,120]{1,2,0:T(8,128)(2,1)}, u32[]{:S(2)}, u32[]{:S(2)}) %all-to-all-start.3) | async-done | bytes 1966112 | tf_op jit(solution)/shard_map/all_to_all | solution.py:81
  430.0 4.3 all-to-all-start.4
  435.2 36.0 %all-gather.22.cloned.1.call-done = bf16[960,1280]{1,0:T(8,128)(2,1)} async-done(((bf16[120,1280]{1,0:T(8,128)(2,1)}), bf16[960,1280]{1,0:T(8,128)(2,1)}) %all-gather.22.cloned.1.call-update) | async-done | bytes 2457616 | tf_op jit(solution)/shard_map/all_gather | solution.py:82
  471.1 7.5 fusion.53
  478.7 45.1 %all-gather.28.cloned.1.call-done = bf16[960,640]{1,0:T(8,128)(2,1)} async-done(((bf16[120,640]{1,0:T(8,128)(2,1)}), bf16[960,640]{1,0:T(8,128)(2,1)}) %all-gather.28.cloned.1.call-update) | async-done | bytes 1228816 | tf_op jit(solution)/shard_map/all_gather | solution.py:82
  523.8 7.3 multiply_convert_fusion.1
  531.1 1.7 pad_maximum_fusion
  532.8 400.4 %all-gather.30.cloned.1.call-done = bf16[8192,1280]{1,0:T(8,128)(2,1)} async-done(((bf16[1024,1280]{1,0:T(8,128)(2,1)}), bf16[8192,1280]{1,0:T(8,128)(2,1)}) %all-gather.30.cloned.1.call-update) | async-done | bytes 20971536 | tf_op jit(solution)/shard_map/all_gather | solution.py:87
  933.3 14.8 convolution_convert_fusion.3
  948.3 30.3 %reduce-scatter.11.cloned.1.call-done = bf16[2048,120]{0,1:T(8,128)(2,1)} async-done(((bf16[8192,120]{0,1:T(8,128)(2,1)}), bf16[2048,120]{0,1:T(8,128)(2,1)}) %reduce-scatter.11.cloned.1.call-update) | async-done | bytes 491536 | tf_op jit(solution)/shard_map/reduce_scatter | solution.py:90
  978.6 2.0 fusion.32
  980.7 32.5 %all-gather.2 = f32[16384]{0:T(1024)} all-gather(f32[2048]{0:T(1024)S(1)} %get-tuple-element.67), channel_id=4, replica_groups=mesh['gx'=8,'gy'=4] {'gx'}, dimensions={0}, use_global_device_ids=true | all-gather | bytes 73728 | tf_op jit(solution)/shard_map/all_gather | solution.py:63
  1013.2 1.5 reshape.325
  1016.9 2.2 fusion.40
  1019.1 22.0 %all-gather.32.cloned.1.call-done = bf16[8192,120]{0,1:T(8,128)(2,1)} async-done(((bf16[2048,120]{0,1:T(8,128)(2,1)}), bf16[8192,120]{0,1:T(8,128)(2,1)}) %all-gather.32.cloned.1.call-update) | async-done | bytes 1966096 | tf_op jit(solution)/shard_map/all_gather | solution.py:80
  1041.1 3.0 copy.128
  1044.1 5.5 all-to-all-start.5
  1049.7 1.6 copy.98
  1051.2 67.3 %all_gather.85 = bf16[960,240]{1,0:T(8,128)(2,1)} all-gather(bf16[120,240]{1,0:T(8,128)(2,1)} %bitcast.221), channel_id=1, replica_groups=mesh['gx'=8,'gy'=4] {'gx'}, dimensions={0}, use_global_device_ids=true | all-gather | bytes 518400 | tf_op jit(solution)/shard_map/all_gather | solution.py:82
  1118.5 2.3 convolution_convert_fusion.5
  1120.9 10.9 all_to_all.138
  1131.7 8.9 fusion.13
  1140.6 7.8 fusion.54
  1148.4 25.3 %fusion.3 = bf16[5,3,256,1024]{2,3,1,0:T(8,128)(2,1)} fusion(f32[5,1024,256,3]{2,1,3,0:T(8,128)} %fusion.54, f32[5,3,256,1024]{2,3,1,0:T(8,128)} %get-tuple-element.97, f32[5,3,256]{2,1,0:T(4,128)S(1)} %log_add_fusion), kind=kOutput, calls=%fused_computation.5 | output fusion | flops 27529984 | bytes 39336960 | tf_op jit(solution)/shard_map/sub | solution.py:202
  1173.7 5.7 convolution_bitcast_fusion
  1180.6 4.7 fusion.39
  1185.5 10.9 all_to_all.139
  1196.4 5.2 reduce-scatter.13.cloned.1.call-done
  1201.6 1.9 pad_maximum_fusion.1
  1204.2 102.1 %all-gather.34.cloned.1.call-done = bf16[8192,400]{0,1:T(8,128)(2,1)} async-done(((bf16[1024,400]{0,1:T(8,128)(2,1)}), bf16[8192,400]{0,1:T(8,128)(2,1)}) %all-gather.34.cloned.1.call-update) | async-done | bytes 6553616 | tf_op jit(solution)/shard_map/all_gather | solution.py:87
  1306.3 5.4 convolution_convert_fusion.1
  1311.8 145.3 %all-gather.24.cloned.1.call-done = bf16[8192,640]{1,0:T(8,128)(2,1)} async-done(((bf16[1024,640]{1,0:T(8,128)(2,1)}), bf16[8192,640]{1,0:T(8,128)(2,1)}) %all-gather.24.cloned.1.call-update) | async-done | bytes 10485776 | tf_op jit(solution)/shard_map/all_gather | solution.py:87
  1457.1 9.3 convolution_convert_fusion.2
  1466.4 7.2 fusion.58
  1473.6 8.9 fusion.57
  1483.4 1.8 fusion.56
  1485.3 1.9 fusion.55
  1490.1 30.5 %all-gather.3 = f32[16384]{0:T(1024)S(1)} all-gather(f32[2048]{0:T(1024)S(1)} %get-tuple-element.69), channel_id=5, replica_groups=mesh['gx'=8,'gy'=4] {'gx'}, dimensions={0}, use_global_device_ids=true | all-gather | bytes 73728 | tf_op jit(solution)/shard_map/all_gather | solution.py:63
  1520.7 6.2 all-reduce
  1526.9 3.0 fusion.26
  (153 shorter events, 20.2 us)
Async XLA Ops:
  7.2 58.5 %all-gather.16.cloned.1.call-start = ((), (), s32[]{:S(2)}) async-start(), calls=%async_computation.14 | async-start | bytes 2457600 | tf_op jit(solution)/shard_map/all_gather | solution.py:80
  68.7 5.7 copy-start.22
  68.7 6.5 copy-start.21
  68.7 6.6 copy-start.16
  68.7 6.6 copy-start.18
  68.7 76.8 %all-to-all-start = ((bf16[8,1024,120]{1,2,0:T(8,128)(2,1)}), bf16[8,1024,120]{1,2,0:T(8,128)(2,1)}, u32[]{:S(2)}, u32[]{:S(2)}) async-start(bf16[8,1024,120]{1,2,0:T(8,128)(2,1)} %bitcast.187), calls=%async_computation | async-start | bytes 3932160 | tf_op jit(solution)/shard_map/all_to_all | solution.py:81
  148.9 24.6 %all-to-all-start.1 = ((bf16[4,256,240]{1,2,0:T(8,128)(2,1)}), bf16[4,256,240]{1,2,0:T(8,128)(2,1)S(1)}, u32[]{:S(2)}, u32[]{:S(2)}) async-start(bf16[4,256,240]{1,2,0:T(8,128)(2,1)} %bitcast.189), calls=%async_computation.1 | async-start | bytes 983040 | tf_op jit(solution)/shard_map/all_to_all | solution.py:97
  152.4 124.0 %all-gather.18.cloned.1.call-start = ((), (), s32[]{:S(2)}) async-start(), calls=%async_computation.15 | async-start | bytes 4423680 | tf_op jit(solution)/shard_map/all_gather | solution.py:87
  188.2 88.2 %copy-start.12 = (bf16[240,120]{1,0:T(8,128)(2,1)S(1)}, bf16[240,120]{1,0:T(8,128)(2,1)}, u32[]{:S(2)}) copy-start(bf16[240,120]{1,0:T(8,128)(2,1)} %param.17) | copy-start | bytes 172804
  207.9 101.8 %copy-start = (bf16[120,2048]{1,0:T(8,128)(2,1)S(1)}, bf16[120,2048]{1,0:T(8,128)(2,1)}, u32[]{:S(2)}) copy-start(bf16[120,2048]{1,0:T(8,128)(2,1)} %param.12) | copy-start | bytes 1474564
  207.9 101.8 %reduce-scatter.7.cloned.1.call-start = ((), (), s32[]{:S(2)}) async-start(), calls=%async_computation.16 | async-start | bytes 2457600 | tf_op jit(solution)/shard_map/reduce_scatter | solution.py:90
  280.5 61.1 %copy-start.23 = (f32[120]{0:T(128)S(1)}, f32[120]{0:T(128)}, u32[]{:S(2)}) copy-start(f32[120]{0:T(128)} %param.18) | copy-start | bytes 1444
  280.5 85.0 %all-gather.20.cloned.1.call-start = ((), (), s32[]{:S(2)}) async-start(), calls=%async_computation.17 | async-start | bytes 2457600 | tf_op jit(solution)/shard_map/all_gather | solution.py:80
  341.5 27.0 %copy-start.20 = (f32[2048]{0:T(1024)}, f32[2048]{0:T(1024)S(1)}, u32[]{:S(2)}) copy-start(f32[2048]{0:T(1024)S(1)} %reduce_sum.112) | copy-start | bytes 24580
  343.6 45.2 %all-gather.26.cloned.1.call-start = ((), (), s32[]{:S(2)}) async-start(), calls=%async_computation.21 | async-start | bytes 2457600 | tf_op jit(solution)/shard_map/all_gather | solution.py:80
  368.5 5.7 copy-start.13
  368.5 5.7 copy-start.14
  368.5 61.5 %all-to-all-start.3 = ((bf16[8,1024,120]{1,2,0:T(8,128)(2,1)}), bf16[8,1024,120]{1,2,0:T(8,128)(2,1)}, u32[]{:S(2)}, u32[]{:S(2)}) async-start(bf16[8,1024,120]{1,2,0:T(8,128)(2,1)} %bitcast.198), calls=%async_computation.4 | async-start | bytes 3932160 | tf_op jit(solution)/shard_map/all_to_all | solution.py:81
  374.2 97.0 %all-gather.22.cloned.1.call-start = ((), (), s32[]{:S(2)}) async-start(), calls=%async_computation.18 | async-start | bytes 2764800 | tf_op jit(solution)/shard_map/all_gather | solution.py:82
  374.3 0.7 copy-start.8
  430.0 93.8 %all-to-all-start.4 = ((bf16[8,1024,120]{1,2,0:T(8,128)(2,1)}), bf16[8,1024,120]{1,2,0:T(8,128)(2,1)}, u32[]{:S(2)}, u32[]{:S(2)}) async-start(bf16[8,1024,120]{1,2,0:T(8,128)(2,1)} %bitcast.197), calls=%async_computation.6 | async-start | bytes 3932160 | tf_op jit(solution)/shard_map/all_to_all | solution.py:81
  434.4 89.4 %all-gather.28.cloned.1.call-start = ((), (), s32[]{:S(2)}) async-start(), calls=%async_computation.22 | async-start | bytes 1382400 | tf_op jit(solution)/shard_map/all_gather | solution.py:82
  435.1 498.1 %all-gather.30.cloned.1.call-start = ((), (), s32[]{:S(2)}) async-start(), calls=%async_computation.23 | async-start | bytes 23592960 | tf_op jit(solution)/shard_map/all_gather | solution.py:87
  532.8 400.5 %copy-start.9 = (bf16[120,1280]{1,0:T(8,128)(2,1)S(1)}, bf16[120,1280]{1,0:T(8,128)(2,1)}, u32[]{:S(2)}) copy-start(bf16[120,1280]{1,0:T(8,128)(2,1)} %copy-done.8) | copy-start | bytes 921604
  532.8 445.9 %copy-start.3 = (bf16[2048,120]{0,1:T(8,128)(2,1)S(1)}, bf16[2048,120]{0,1:T(8,128)(2,1)}, u32[]{:S(2)}) copy-start(bf16[2048,120]{0,1:T(8,128)(2,1)} %reduce-scatter.7.cloned.1.call-done) | copy-start | bytes 1474564
  532.8 445.8 %reduce-scatter.11.cloned.1.call-start = ((), (), s32[]{:S(2)}) async-start(), calls=%async_computation.24 | async-start | bytes 2457600 | tf_op jit(solution)/shard_map/reduce_scatter | solution.py:90
  948.1 68.8 %copy-start.6 = (bf16[120,2048]{1,0:T(8,128)(2,1)S(1)}, bf16[120,2048]{1,0:T(8,128)(2,1)}, u32[]{:S(2)}) copy-start(bf16[120,2048]{1,0:T(8,128)(2,1)} %param.23) | copy-start | bytes 1474564
  948.1 93.0 %all-gather.32.cloned.1.call-start = ((), (), s32[]{:S(2)}) async-start(), calls=%async_computation.25 | async-start | bytes 2457600 | tf_op jit(solution)/shard_map/all_gather | solution.py:80
  1044.1 74.4 %all-to-all-start.5 = ((bf16[8,1024,120]{1,2,0:T(8,128)(2,1)}), bf16[8,1024,120]{1,2,0:T(8,128)(2,1)}, u32[]{:S(2)}, u32[]{:S(2)}) async-start(bf16[8,1024,120]{1,2,0:T(8,128)(2,1)} %bitcast.199), calls=%async_computation.8 | async-start | bytes 3932160 | tf_op jit(solution)/shard_map/all_to_all | solution.py:81
  1049.6 146.8 %reduce-scatter.15.cloned.1.call-start = ((), (), s32[]{:S(2)}) async-start(), calls=%async_computation.27 | async-start | bytes 819200 | tf_op jit(solution)/shard_map/reduce_scatter | solution.py:212
  1148.3 53.3 %reduce-scatter.13.cloned.1.call-start = ((), (), s32[]{:S(2)}) async-start(), calls=%async_computation.26 | async-start | bytes 819200 | tf_op jit(solution)/shard_map/reduce_scatter | solution.py:209
  1173.7 5.7 copy-start.11
  1180.5 4.7 copy-start.15
  1180.5 125.8 %all-gather.34.cloned.1.call-start = ((), (), s32[]{:S(2)}) async-start(), calls=%async_computation.28 | async-start | bytes 7372800 | tf_op jit(solution)/shard_map/all_gather | solution.py:87
  1196.3 110.0 %copy-start.17 = (bf16[120,80]{0,1:T(8,128)(2,1)S(1)}, bf16[120,80]{0,1:T(8,128)(2,1)}, u32[]{:S(2)}) copy-start(bf16[120,80]{0,1:T(8,128)(2,1)} %param.16) | copy-start | bytes 57604
  1196.3 110.0 %copy-start.19 = (bf16[120,80]{0,1:T(8,128)(2,1)S(1)}, bf16[120,80]{0,1:T(8,128)(2,1)}, u32[]{:S(2)}) copy-start(bf16[120,80]{0,1:T(8,128)(2,1)} %param.15) | copy-start | bytes 57604
  1203.6 253.5 %all-gather.24.cloned.1.call-start = ((), (), s32[]{:S(2)}) async-start(), calls=%async_computation.19 | async-start | bytes 11796480 | tf_op jit(solution)/shard_map/all_gather | solution.py:87
  1204.2 252.9 %copy-start.10 = (bf16[640,120]{0,1:T(8,128)(2,1)S(1)}, bf16[640,120]{0,1:T(8,128)(2,1)}, u32[]{:S(2)}) copy-start(bf16[640,120]{0,1:T(8,128)(2,1)} %param.21) | copy-start | bytes 460804
  1204.2 284.4 %reduce-scatter.17.cloned.1.call-start = ((), (), s32[]{:S(2)}) async-start(), calls=%async_computation.29 | async-start | bytes 2457600 | tf_op jit(solution)/shard_map/reduce_scatter | solution.py:90
  1311.8 215.1 %reduce-scatter.9.cloned.1.call-start = ((), (), s32[]{:S(2)}) async-start(), calls=%async_computation.20 | async-start | bytes 2457600 | tf_op jit(solution)/shard_map/reduce_scatter | solution.py:90
  1466.4 7.2 copy-start.4
  1466.4 18.8 %slice-start = ((s8[6553600]{0:T(1024)(128)(4,1)}), s8[4194304]{0:T(1024)(128)(4,1)S(1)}, s32[]{:S(2)}) async-start(s8[6553600]{0:T(1024)(128)(4,1)} %bitcast.190), calls=%async_computation.30 | async-start | bytes 8388608
  1473.6 9.8 copy-start.1
  1473.6 9.8 copy-start.5
  1473.6 11.6 slice-start.1
  1483.4 1.8 copy-start.2
  1485.2 3.4 copy-start.25
  1485.2 35.4 %copy-start.26 = (f32[120]{0:T(128)S(1)}, f32[120]{0:T(128)}, u32[]{:S(2)}) copy-start(f32[120]{0:T(128)} %get-tuple-element.66) | copy-start | bytes 1444
  1485.2 41.6 %copy-start.7 = (bf16[2048,120]{0,1:T(8,128)(2,1)S(1)}, bf16[2048,120]{0,1:T(8,128)(2,1)}, u32[]{:S(2)}) copy-start(bf16[2048,120]{0,1:T(8,128)(2,1)} %reduce-scatter.11.cloned.1.call-done) | copy-start | bytes 1474564
  1485.2 41.6 %copy-start.24 = (f32[120]{0:T(128)S(1)}, f32[120]{0:T(128)}, u32[]{:S(2)}) copy-start(f32[120]{0:T(128)} %param.18) | copy-start | bytes 1444
Sparse Core Ops, SparseCore 0:
  42.9 22.7 all-gather.15
  208.0 68.2 all-gather.17
  280.6 28.9 reduce-scatter.6
  343.7 21.7 all-gather.19
  366.9 21.8 all-gather.25
  391.4 79.7 all-gather.21
  473.3 50.4 all-gather.27
  532.9 400.3 all-gather.29
  948.2 30.3 reduce-scatter.10
  1019.2 21.7 all-gather.31
  1148.5 20.9 reduce-scatter.14
  1180.7 20.9 reduce-scatter.12
  1204.4 101.8 all-gather.33
  1308.3 148.6 all-gather.23
  1459.5 28.5 reduce-scatter.16
  1490.5 30.3 reduce-scatter.8
